TPU v7x, 32 devices: a whole 2x2x4 slice. The times are simulated.
32 devices in a mesh: rep: 4 (over z), exp: 4 (over x, core), shard: 2 (over y).
Axes of the slice: x: 2, y: 2, z: 4, core: 2. Of those that a mesh axis runs over, the one named last changes fastest.
Arguments:
- tokens: bfloat16 [3584, 2048], P(('rep', 'exp', 'shard')), may hold values from -1.5 to 1.5
- routes: int32 [3584, 2], P(('rep', 'exp', 'shard')), may hold values from 0 to 3, all different within a row; in each aligned block of 112 rows (0 to 111, 112 to 223, ...) at most 63 rows name the same one
- gate_weight: bfloat16 [4, 2048, 7168], P('exp', None, 'shard'), may hold values from -0.125 to 0.125
- gate_cotangent: bfloat16 [4, 2016, 7168], P('exp', 'rep', 'shard'), may hold values from -0.75 to 0.75
Outputs:
- token_grad: bfloat16 [3584, 2048], P(('rep', 'exp', 'shard'))
- weight_grad: bfloat16 [4, 2048, 7168], P('exp', None, 'shard')
Inputs may be any that keep to these rules, and one draw needn't show every extreme that they name: `routes`: the two entries of a row differ. The rows of one device name one expert at most 63 times, and some device names some expert exactly 63 times.
All inputs are finite; a program needn't handle non-finite values.
Results may differ from a plain program's by a relative error of at most 0.015.
Values may be sent and summed in bfloat16 or wider, within the bound.
A program may use at most 128 MiB of HBM per device.

v0:
```python
import jax
import jax.numpy as jnp
from jax import lax
from jax.sharding import PartitionSpec as P


def slot_matrix(route_rows, experts, slot_cap):
    expert_ids = jnp.arange(experts, dtype=jnp.int32)
    onehot = (route_rows[:, :, None] == expert_ids[None, None, :]).astype(jnp.int32)
    flattened = onehot.reshape(-1, experts)
    before = jnp.cumsum(flattened, axis=0) - flattened
    position = jnp.sum(before * flattened, axis=1)
    target = jnp.sum(flattened * expert_ids[None, :], axis=1) * slot_cap + position
    slot_ids = jnp.arange(experts * slot_cap, dtype=jnp.int32)
    matches = (target[None, :] == slot_ids[:, None]).astype(jnp.int32)
    return matches.reshape(experts * slot_cap, -1, 2).sum(axis=2)


def body(tokens, routes, gate_weight, gate_cotangent):
    experts = lax.axis_size("exp")
    shards = lax.axis_size("shard")
    features = tokens.shape[1]
    cotangent = gate_cotangent[0]
    hidden = cotangent.shape[1]
    slot_cap = cotangent.shape[0] // (experts * shards)
    weight = gate_weight[0]
    blocks = cotangent.reshape(experts, shards, slot_cap, hidden)
    placing = slot_matrix(routes, experts, slot_cap).astype(jnp.bfloat16)
    outgoing = jnp.dot(placing, tokens, preferred_element_type=jnp.float32).astype(jnp.bfloat16)
    outgoing = outgoing.reshape(experts, slot_cap, features)
    contract_rows = (((0,), (0,)), ((), ()))
    copies = jnp.broadcast_to(outgoing[:, None], (experts, shards, slot_cap, features))
    copies = copies.reshape(experts * shards, slot_cap, features)
    arrived = lax.all_to_all(copies, ("exp", "shard"), split_axis=0, concat_axis=0, tiled=True)
    partial_grad = lax.dot_general(
        arrived.reshape(-1, features), cotangent, contract_rows, preferred_element_type=jnp.float32
    )
    weight_grad = lax.psum(partial_grad.astype(jnp.bfloat16), "rep")[None]
    ordered = jnp.swapaxes(blocks, 0, 1).reshape(-1, hidden)
    summed = lax.psum_scatter(
        lax.dot_general(
            ordered, weight, (((1,), (1,)), ((), ())), preferred_element_type=jnp.float32
        ).astype(jnp.bfloat16),
        "shard",
        scatter_dimension=0,
        tiled=True,
    )
    slot_grad = summed.reshape(experts, slot_cap, features)
    returned = lax.all_to_all(slot_grad, "exp", split_axis=0, concat_axis=0, tiled=True)
    token_grad = jnp.dot(
        placing.T, returned.reshape(-1, features), preferred_element_type=jnp.float32
    )
    return (token_grad.astype(jnp.bfloat16), weight_grad)


def solution(mesh):
    placed = (
        P(("rep", "exp", "shard"), None),
        P(("rep", "exp", "shard"), None),
        P("exp", None, "shard"),
        P("exp", "rep", "shard"),
    )
    return jax.shard_map(
        body,
        mesh=mesh,
        in_specs=placed,
        out_specs=(P(("rep", "exp", "shard"), None), P("exp", None, "shard")),
        check_vma=False,
    )
```

profile of v0, /device:TPU:0, one launch (start us, length us, event | category | flops | bytes accessed | tf_op | source)
XLA Modules:
  0.0 571.3 jit_solution(2415380312625847076)
XLA Ops:
  7.2 0.0 copy-start
  7.2 0.0 all-reduce.5.cloned.1.call-start
  7.2 0.8 copy.16
  8.1 0.1 eq.37
  8.2 1.2 reduce-window.6
  9.5 0.1 slice.12
  9.5 0.1 copy.17
  9.7 0.1 copy.18
  9.8 0.1 add_bitcast_fusion
  9.9 0.1 add.15
  10.0 0.1 copy.19
  10.1 0.1 convert_reduce_fusion
  10.2 0.0 copy-done
  10.2 0.5 convolution_convert_fusion.1
  10.7 0.3 broadcast_in_dim.6
  11.0 0.2 broadcast_in_dim.7
  11.2 30.7 %all_to_all.10 = bf16[8,63,2048]{2,1,0:T(8,128)(2,1)S(1)} all-to-all(bf16[8,63,2048]{2,1,0:T(8,128)(2,1)S(1)} %bitcast.29), channel_id=1, replica_groups=mesh['rep'=4,'exp'=4,'shard'=2] {'exp','shard'}, dimensions={0} | all-to-all | bytes 4128768 | tf_op jit(solution)/shard_map/all_to_all | solution.py:34
  41.9 2.0 reshape.61
  43.8 13.3 %fusion.3 = bf16[1,2048,3584]{2,1,0:T(8,128)(2,1)} fusion(bf16[504,2048]{1,0:T(8,128)(2,1)} %reshape.61, bf16[1,504,3584]{2,1,0:T(8,128)(2,1)} %param.7), kind=kOutput, calls=%fused_computation.3 | convolution fusion | flops 7406092288 | bytes 20357120 | tf_op jit(solution)/shard_map/dot_general | solution.py:35
  57.1 0.0 all-reduce.5.cloned.1.call-update
  57.2 4.9 reshape_squeeze.3
  62.1 5.2 copy.20
  67.2 4.9 reshape.57
  72.2 0.0 copy-start.2
  72.2 13.0 %fusion.5 = bf16[504,2048]{1,0:T(8,128)(2,1)} fusion(bf16[504,3584]{1,0:T(8,128)(2,1)} %reshape.57, bf16[1,2048,3584]{2,1,0:T(8,128)(2,1)} %param.6), kind=kOutput, calls=%fused_computation.5 | convolution fusion | flops 7399784448 | bytes 20357120 | tf_op jit(solution)/shard_map/dot_general | solution.py:41
  85.2 28.6 %fusion = bf16[256,2048]{1,0:T(8,128)(2,1)S(1)} fusion(bf16[504,2048]{1,0:T(8,128)(2,1)} %fusion.5), kind=kCustom, calls=%all-reduce-scatter | all-reduce-scatter fusion | flops 1048577 | bytes 3113472
  113.8 3.6 collective-permute-start
  117.5 0.0 copy-done.2
  117.5 0.6 dynamic-slice.4
  118.7 0.2 collective-permute-done
  118.9 1.2 concatenate
  120.1 0.3 constant_dynamic-slice_fusion
  120.4 0.3 reshape.58
  120.7 17.6 %all_to_all.11 = bf16[4,63,2048]{2,1,0:T(8,128)(2,1)} all-to-all(bf16[4,63,2048]{2,1,0:T(8,128)(2,1)S(1)} %reshape.58), channel_id=1, replica_groups=mesh['rep'=4,'exp'=4,'shard'=2] {'exp'}, dimensions={0} | all-to-all | bytes 2064384 | tf_op jit(solution)/shard_map/all_to_all | solution.py:49
  138.3 1.5 reshape.59
  139.8 1.1 convolution_convert_fusion.2
  140.9 410.5 %all-reduce.5.cloned.1.call-done = bf16[1,2048,3584]{2,1,0:T(8,128)(2,1)} async-done(((bf16[1,2048,3584]{2,1,0:T(8,128)(2,1)}), bf16[1,2048,3584]{2,1,0:T(8,128)(2,1)}) %all-reduce.5.cloned.1.call-update) | async-done | bytes 14680080 | tf_op jit(solution)/shard_map/psum | solution.py:38
  551.3 0.0 copy-start.1
  551.3 13.2 %copy.25 = bf16[1,2048,3584]{2,1,0:T(8,128)(2,1)} copy(bf16[1,2048,3584]{2,1,0:T(8,128)(2,1)} %all-reduce.5.cloned.1.call-done) | data formatting | bytes 29360128
  564.5 0.0 copy-done.1
  (9 shorter events, 0.1 us)
Async XLA Ops:
  7.2 3.1 copy-start
  7.2 544.1 %all-reduce.5.cloned.1.call-start = ((), (), s32[]{:S(2)}) async-start(), calls=%async_computation.2 | async-start | bytes 29360128 | tf_op jit(solution)/shard_map/psum | solution.py:38
  72.2 45.3 %copy-start.2 = (u32[32]{0:T(128)S(1)}, u32[32]{0:T(128)}, u32[]{:S(2)}) copy-start(u32[32]{0:T(128)} %constant.19) | copy-start | bytes 388
  113.8 5.1 collective-permute-start
  551.3 13.2 %copy-start.1 = (bf16[112,2048]{1,0:T(8,128)(2,1)S(1)}, bf16[112,2048]{1,0:T(8,128)(2,1)}, u32[]{:S(2)}) copy-start(bf16[112,2048]{1,0:T(8,128)(2,1)} %param.4) | copy-start | bytes 1376260
Sparse Core Ops, SparseCore 0:
  57.3 493.9 all-reduce.4
where the time goes:
time: 572 us; the launch traced here: 571 us
  waiting for transfers between devices  411 us (72%)
  blocking collectives  76.8 us (13%)
  local copies, waits for them, and re-layouts  36 us (6%)
  matrix products  27.9 us (5%)
  between operations  14.8 us (3%)
    psum x1, waiting for transfers between devices, body(): weight_grad = lax.psum(partial_grad.astype(jnp.bfloat16), 'rep')[None]  410 us
    all_to_all x1, blocking collectives, body(): lax.all_to_all(copies, ('exp', 'shard'), split_axis=0, concat_axis=0, til...  30.7 us
    unnamed x1, blocking collectives  28.6 us
    all_to_all x1, blocking collectives, body(): lax.all_to_all(slot_grad, 'exp', split_axis=0, concat_axis=0, tiled=True)  17.6 us
    unnamed x13, local copies, waits for them, and re-layouts  16.1 us
    dot_general x1, matrix products, body(): lax.dot_general(arrived.reshape(-1, features), cotangent, contract_rows,...  13.3 us
    dot_general x1, matrix products, body(): lax.dot_general(ordered, weight, (((1,), (1,)), ((), ())), preferred_elem...  13 us
  transfers between devices with their start and end apart: 2, of which 2 were waited for; matrix products, arithmetic and copies ran while one was open for 11% of the time, Pallas kernels for 0%

commit v1 on v0

--- a/solution.py
+++ b/solution.py
@@ -2,6 +2,11 @@
 import jax.numpy as jnp
 from jax import lax
 from jax.sharding import PartitionSpec as P
+
+
+def summed_here(shard, mesh_axis):
+    shards = lax.all_gather(shard, mesh_axis)
+    return jnp.sum(shards, axis=0)
 
 
 def slot_matrix(route_rows, experts, slot_cap):
@@ -35,7 +40,7 @@
     partial_grad = lax.dot_general(
         arrived.reshape(-1, features), cotangent, contract_rows, preferred_element_type=jnp.float32
     )
-    weight_grad = lax.psum(partial_grad.astype(jnp.bfloat16), "rep")[None]
+    weight_grad = summed_here(partial_grad.astype(jnp.bfloat16), "rep")[None]
     ordered = jnp.swapaxes(blocks, 0, 1).reshape(-1, hidden)
     summed = lax.psum_scatter(
         lax.dot_general(

time: 572 us -> 1070 us (1.87)
  waiting for transfers between devices: 411 us -> 886 us
  other arithmetic: 1.5 us -> 29.1 us
  local copies, waits for them, and re-layouts: 36 us -> 24.8 us
    all_gather x0 -> x1, waiting for transfers between devices: none -> 886 us  [summed_here(): shards = lax.all_gather(shard, mesh_axis)]
    psum x1 -> x0, waiting for transfers between devices: 410 us -> none  [body(): weight_grad = lax.psum(partial_grad.astype(jnp.bfloat16), 'rep')[None]]
    reduce_sum x0 -> x1, other arithmetic: none -> 27.6 us  [summed_here(): return jnp.sum(shards, axis=0)]
    unnamed x13 -> x12, local copies, waits for them, and re-layouts: 16.1 us -> 2.95 us
  transfers between devices with their start and end apart: 2 -> 2, of which waited for: 2 -> 1; matrix products, arithmetic and copies ran while one was open for 11% -> 6% of each run, Pallas kernels for 0% -> 0%
where the time goes in v1:
time: 1070 us
  waiting for transfers between devices  886 us (83%)
  blocking collectives  77.2 us (7%)
  matrix products  30.9 us (3%)
  other arithmetic  29.1 us (3%)
  local copies, waits for them, and re-layouts  24.8 us (2%)
  between operations  14.8 us (1%)
    all_gather x1, waiting for transfers between devices, summed_here(): shards = lax.all_gather(shard, mesh_axis)  886 us
    all_to_all x1, blocking collectives, body(): lax.all_to_all(copies, ('exp', 'shard'), split_axis=0, concat_axis=0, til...  30.7 us
    unnamed x1, blocking collectives  28.9 us
    reduce_sum x1, other arithmetic, summed_here(): return jnp.sum(shards, axis=0)  27.6 us
  transfers between devices with their start and end apart: 2, of which 1 were waited for; matrix products, arithmetic and copies ran while one was open for 6% of the time, Pallas kernels for 0%

profile of v1, /device:TPU:0, one launch (start us, length us, event | category | flops | bytes accessed | tf_op | source)
XLA Modules:
  0.0 1066.4 jit_solution(10015116792229170456)
XLA Ops:
  7.2 0.0 copy-start
  7.2 0.0 all-gather.3.cloned.1.call-start
  7.2 0.8 copy.16
  8.1 0.1 eq.37
  8.2 1.2 reduce-window.6
  9.5 0.1 slice.12
  9.5 0.1 copy.17
  9.7 0.1 copy.18
  9.8 0.1 add_bitcast_fusion
  9.9 0.1 add.13
  10.0 0.1 copy.19
  10.1 0.1 convert_reduce_fusion
  10.2 0.0 copy-done
  10.2 0.5 convolution_convert_fusion.1
  10.7 0.3 broadcast_in_dim.6
  11.0 0.2 broadcast_in_dim.7
  11.2 30.7 %all_to_all.10 = bf16[8,63,2048]{2,1,0:T(8,128)(2,1)S(1)} all-to-all(bf16[8,63,2048]{2,1,0:T(8,128)(2,1)S(1)} %bitcast.31), channel_id=1, replica_groups=mesh['rep'=4,'exp'=4,'shard'=2] {'exp','shard'}, dimensions={0} | all-to-all | bytes 4128768 | tf_op jit(solution)/shard_map/all_to_all | solution.py:39
  41.9 2.0 reshape.61
  43.8 13.3 %convolution_convert_fusion = bf16[2048,3584]{1,0:T(8,128)(2,1)} fusion(bf16[504,2048]{1,0:T(8,128)(2,1)} %reshape.61, bf16[1,504,3584]{2,1,0:T(8,128)(2,1)} %param.7), kind=kOutput, calls=%fused_computation | convolution fusion | flops 7406092288 | bytes 20357120 | tf_op jit(solution)/shard_map/dot_general | solution.py:40
  57.1 0.0 all-gather.3.cloned.1.call-update
  57.2 4.9 reshape_squeeze.3
  62.1 4.7 copy.20
  66.8 7.3 reshape.57
  74.1 0.0 copy-start.2
  74.1 16.1 %fusion.4 = bf16[504,2048]{1,0:T(8,128)(2,1)} fusion(bf16[504,3584]{1,0:T(8,128)(2,1)} %reshape.57, bf16[1,2048,3584]{2,1,0:T(8,128)(2,1)} %param.6), kind=kOutput, calls=%fused_computation.4 | convolution fusion | flops 7399784448 | bytes 20357120 | tf_op jit(solution)/shard_map/dot_general | solution.py:46
  90.2 28.9 %fusion = bf16[256,2048]{1,0:T(8,128)(2,1)S(1)} fusion(bf16[504,2048]{1,0:T(8,128)(2,1)} %fusion.4), kind=kCustom, calls=%all-reduce-scatter | all-reduce-scatter fusion | flops 1048577 | bytes 3113472
  119.2 3.7 collective-permute-start
  122.9 0.0 copy-done.2
  122.9 0.6 dynamic-slice.4
  124.2 0.0 collective-permute-done
  124.2 1.2 concatenate
  125.4 0.3 constant_dynamic-slice_fusion
  125.7 0.3 reshape.58
  126.0 17.6 %all_to_all.11 = bf16[4,63,2048]{2,1,0:T(8,128)(2,1)} all-to-all(bf16[4,63,2048]{2,1,0:T(8,128)(2,1)S(1)} %reshape.58), channel_id=1, replica_groups=mesh['rep'=4,'exp'=4,'shard'=2] {'exp'}, dimensions={0} | all-to-all | bytes 2064384 | tf_op jit(solution)/shard_map/all_to_all | solution.py:54
  143.5 1.5 reshape.59
  145.1 1.1 convolution_convert_fusion.2
  146.1 885.8 %all-gather.3.cloned.1.call-done = bf16[8192,3584]{1,0:T(8,128)(2,1)} async-done(((bf16[2048,3584]{1,0:T(8,128)(2,1)}), bf16[8192,3584]{1,0:T(8,128)(2,1)}) %all-gather.3.cloned.1.call-update) | async-done | bytes 58720272 | tf_op jit(solution)/shard_map/all_gather | solution.py:8
  1032.0 0.0 copy-start.1
  1032.0 27.6 %reduce_sum.42 = bf16[2048,3584]{1,0:T(8,128)(2,1)} reduce(bf16[4,2048,3584]{2,1,0:T(8,128)(2,1)} %bitcast.28, bf16[]{:T(256)} %constant.13.clone.1), dimensions={0}, to_apply=%region_6.7 | reduce | flops 22020096 | bytes 73400320 | tf_op jit(solution)/shard_map/reduce_sum | solution.py:9
  1059.6 0.0 copy-done.1
  (9 shorter events, 0.1 us)
Async XLA Ops:
  7.2 3.1 copy-start
  7.2 1024.8 %all-gather.3.cloned.1.call-start = ((), (), s32[]{:S(2)}) async-start(), calls=%async_computation.2 | async-start | bytes 73400320 | tf_op jit(solution)/shard_map/all_gather | solution.py:8
  74.1 48.8 %copy-start.2 = (u32[32]{0:T(128)S(1)}, u32[32]{0:T(128)}, u32[]{:S(2)}) copy-start(u32[32]{0:T(128)} %constant.22) | copy-start | bytes 388
  119.2 5.0 collective-permute-start
  1032.0 27.6 %copy-start.1 = (bf16[112,2048]{1,0:T(8,128)(2,1)S(1)}, bf16[112,2048]{1,0:T(8,128)(2,1)}, u32[]{:S(2)}) copy-start(bf16[112,2048]{1,0:T(8,128)(2,1)} %param.4) | copy-start | bytes 1376260
Sparse Core Ops, SparseCore 0:
  57.3 974.6 all-gather.2
